TPU v7x, 128 devices: a whole 4x4x4 slice. The times are simulated.
128 devices in a mesh: stn: 16 (over y_lo, z, core), chan: 8 (over y_hi, x).
Axes of the slice: x: 4, y: 4 (y_hi: 2, y_lo: 2; y = y_hi * 2 + y_lo), z: 4, core: 2. Of those that a mesh axis runs over, the one named last changes fastest.
Arguments:
- voltages: bfloat16 [16, 2, 256, 131072], P('stn', None, None, 'chan'), may hold values from -6 to 6
- positions: float32 [16, 3, 256], P('stn'), may hold values from -4 to 4
- directions: float32 [3, 64], replicated, may hold values from -0.5 to 0.5
- flag_mask: int32 [16, 2, 2048], P('stn', None, 'chan'), may hold values from 0 to 1, as said below
- tapers: float32 [16, 8], P('stn'), may hold values from 0.3 to 3
- weight_index: int32 [16, 64], P('stn'), may hold values from 0 to 7
Outputs:
- beam_power: float32 [64, 131072], P('stn', 'chan')
- beam_total: float32 [64], P('stn')
Inputs may be any that keep to these rules, and one draw needn't show every extreme that they name: `flag_mask`: the first block of station 0 is kept in every channel.
All inputs are finite; a program needn't handle non-finite values.
Results may differ from a plain program's by a relative error of at most 0.003.
Values sent between devices are 32-bit elements; how exact they have to be, the bound alone decides.
No kernel may reach another device: no remote copies, remote signals or barrier semaphores. Data moves between devices by JAX's collectives and lax.ppermute only.
A program may use at most 192 MiB of HBM per device.

v0:
```python
import math

import jax
import jax.numpy as jnp
from jax import lax
from jax.sharding import PartitionSpec as P

BLOCK = 128


def from_everyone(array, axis):
    devices = lax.axis_size(axis)
    return lax.all_to_all(
        jnp.broadcast_to(array[None], (devices, *array.shape)), axis, 0, 0, tiled=True
    )


def of_everyone(array, axis):
    return from_everyone(array, axis).sum(axis=0)


def station_beam(volts, place, keep_flags, weight_row, directions, ratio):
    delay = (
        directions[0][:, None] * place[0][None, :]
        + directions[1][:, None] * place[1][None, :]
        + directions[2][:, None] * place[2][None, :]
    )
    phase = 2.0 * math.pi * delay[:, :, None] * ratio[None, None, :]
    blocks = keep_flags.shape[0]
    chan_local = keep_flags.shape[1]
    keep = jnp.broadcast_to(
        keep_flags.astype(jnp.float32)[:, None, :], (blocks, BLOCK, chan_local)
    ).reshape(blocks * BLOCK, chan_local)
    amplitude = weight_row[:, None, None] * keep[None, :, :]
    steer_real = (amplitude * jnp.cos(phase)).astype(jnp.bfloat16)
    steer_imag = (-amplitude * jnp.sin(phase)).astype(jnp.bfloat16)
    upper = jnp.concatenate((steer_real, -steer_imag), axis=1)
    lower = jnp.concatenate((steer_imag, steer_real), axis=1)
    steer_block = jnp.concatenate((upper, lower), axis=0)
    signal = volts.reshape(2 * volts.shape[1], chan_local, -1)
    return jnp.einsum("pkc,kct->pct", steer_block, signal, preferred_element_type=jnp.float32)


def on_device(voltages, positions, directions, flag_mask, tapers, weight_index):
    chan_local = flag_mask.shape[2]
    beam_count = directions.shape[1]
    first_channel = lax.axis_index("chan") * chan_local
    chan_whole = chan_local * lax.axis_size("chan")
    ratio = (first_channel + jnp.arange(chan_local)).astype(jnp.float32) / chan_whole
    ratio = 1.0 + 0.5 * ratio
    choose = (weight_index[:, :, None] == jnp.arange(tapers.shape[1])[None, None, :]).astype(
        jnp.float32
    )
    station_weight = jnp.sum(choose * tapers[:, None, :], axis=2)
    alive = jnp.sum(flag_mask, axis=1).astype(jnp.float32) * BLOCK
    counts = jnp.dot(station_weight.T, alive, precision=lax.Precision.HIGHEST)
    partial_value = station_beam(
        voltages[0], positions[0], flag_mask[0], station_weight[0], directions, ratio
    )
    partial_value = partial_value.reshape(2, beam_count, -1).transpose(1, 0, 2)
    rows = beam_count // lax.axis_size("stn")
    summed, counts_all = lax.psum((partial_value, counts), "stn")
    start = lax.axis_index("stn") * rows
    mine = lax.dynamic_slice_in_dim(summed, start, rows, 0)
    counts_mine = lax.dynamic_slice_in_dim(counts_all, start, rows, 0)
    scaled = mine.reshape(rows, 2, chan_local, -1) / counts_mine[:, None, :, None]
    power = scaled[:, 0] * scaled[:, 0] + scaled[:, 1] * scaled[:, 1]
    beam_power = power.reshape(rows, -1)
    beam_total = of_everyone(jnp.sum(beam_power, axis=1), "chan")
    return (beam_power, beam_total)


def solution(mesh):
    in_specs = (
        P("stn", None, None, "chan"),
        P("stn", None, None),
        P(),
        P("stn", None, "chan"),
        P("stn", None),
        P("stn", None),
    )
    out_specs = (P("stn", "chan"), P("stn"))
    return jax.shard_map(
        on_device, mesh=mesh, in_specs=in_specs, out_specs=out_specs, check_vma=False
    )
```

profile of v0, /device:TPU:0, one launch (start us, length us, event | category | flops | bytes accessed | tf_op | source)
XLA Modules:
  0.0 434.2 jit_solution(10863415431828390754)
XLA Ops:
  7.2 0.0 all-reduce.3.cloned.1.call-start
  7.2 0.7 fusion.19
  7.9 0.8 slice_bitcast_fusion.2
  8.7 0.8 fusion.20
  9.5 0.1 copy.18
  9.7 0.3 broadcast_in_dim.4
  10.0 0.8 select_reduce_fusion
  10.8 0.1 add_multiply_fusion
  10.9 63.9 %fusion.10 = (bf16[64,256,256]{1,0,2:T(8,128)(2,1)}, bf16[64,256,256]{1,0,2:T(8,128)(2,1)}) fusion(f32[256]{0:T(256)S(1)} %multiply_add_fusion, f32[64,256]{1,0:T(8,128)S(1)} %add_multiply_fusion, f32[256,256]{0,1:T(8,128)S(1)} %bitcast.30, f32[64]{0:T(128)S(1)} %select_reduce_fusion), kind=kLoop, calls=%fused_computation.14 | loop fusion | flops 29360128 | bytes 17106176 | tf_op jit(solution)/shard_map/convert_element_type | solution.py:36
  74.7 59.0 %fusion.16 = bf16[64,256,256]{1,0,2:T(8,128)(2,1)} fusion(f32[256]{0:T(256)S(1)} %multiply_add_fusion, f32[64,256]{1,0:T(8,128)S(1)} %add_multiply_fusion, f32[256,256]{0,1:T(8,128)S(1)} %bitcast.31, f32[64]{0:T(128)S(1)} %select_reduce_fusion), kind=kLoop, calls=%fused_computation.34 | loop fusion | flops 33554432 | bytes 8717568 | tf_op jit(solution)/shard_map/neg | solution.py:37
  133.8 40.7 %copy.19 = bf16[1,2,256,16384]{2,1,3,0:T(2,128)(2,1)} copy(bf16[1,2,256,16384]{3,2,1,0:T(8,128)(2,1)} %param.6) | data formatting | bytes 33554432 | tf_op args[0]
  174.5 26.9 %reshape_squeeze.3 = bf16[512,256,64]{0,2,1:T(8,128)(2,1)} reshape(bf16[1,2,256,16384]{2,1,3,0:T(2,128)(2,1)} %copy.19) | data formatting | bytes 33554432 | tf_op jit(solution)/shard_map/reshape;squeeze | solution.py:40
  201.4 23.3 %fusion.11 = f32[128,256,64]{0,2,1:T(8,128)} fusion(bf16[512,256,64]{0,2,1:T(8,128)(2,1)} %reshape_squeeze.3, bf16[64,256,256]{1,0,2:T(8,128)(2,1)} %get-tuple-element.7, bf16[64,256,256]{1,0,2:T(8,128)(2,1)} %get-tuple-element.6, bf16[64,256,256]{1,0,2:T(8,128)(2,1)} %fusion.16), kind=kOutput, calls=%fused_computation.15 | convolution fusion | flops 2281701376 | bytes 50331648 | tf_op jit(solution)/shard_map/pkc,kct->pct/dot_general | solution.py:41
  224.6 16.9 %reshape.231 = f32[2,64,16384]{1,0,2:T(2,128)} reshape(f32[128,256,64]{0,2,1:T(8,128)} %fusion.11) | data formatting | bytes 16777216 | tf_op jit(solution)/shard_map/reshape | solution.py:60
  241.5 20.4 %copy.23 = f32[2,64,16384]{2,1,0:T(8,128)} copy(f32[2,64,16384]{1,0,2:T(2,128)} %reshape.231) | data formatting | bytes 16777216 | tf_op jit(solution)/shard_map/reshape | solution.py:60
  262.0 0.7 broadcast_multiply_fusion
  262.7 0.0 all-reduce.3.cloned.1.call-update
  262.7 145.9 %all-reduce.3.cloned.1.call-done = (f32[64,2,16384]{2,0,1:T(8,128)}, f32[64,256]{1,0:T(8,128)}) async-done(((f32[64,2,16384]{2,0,1:T(8,128)}, f32[64,256]{1,0:T(8,128)}), (f32[64,2,16384]{2,0,1:T(8,128)}, f32[64,256]{1,0:T(8,128)})) %all-reduce.3.cloned.1.call-update) | async-done | bytes 8454160 | tf_op jit(solution)/shard_map/psum | solution.py:62
  408.6 1.3 constant_dynamic-slice_fusion.1
  409.9 0.4 copy.21
  410.4 0.6 reshape.230
  411.0 0.7 constant_dynamic-slice_fusion
  411.7 0.2 broadcast_divide_fusion
  411.9 0.2 fusion.17
  412.1 0.6 broadcast_in_dim.5
  412.7 6.4 %all-to-all-start = ((f32[8,1,4]{2,1,0:T(1,128)}), f32[8,1,4]{2,1,0:T(1,128)S(1)}, u32[]{:S(2)}, u32[]{:S(2)}) async-start(f32[8,1,4]{2,1,0:T(1,128)} %broadcast_in_dim.5), calls=%async_computation | async-start | bytes 8192 | tf_op jit(solution)/shard_map/all_to_all | solution.py:13
  419.1 0.9 add.58
  420.1 6.8 %all-to-all-done = f32[8,1,4]{2,1,0:T(1,128)S(1)} async-done(((f32[8,1,4]{2,1,0:T(1,128)}), f32[8,1,4]{2,1,0:T(1,128)S(1)}, u32[]{:S(2)}, u32[]{:S(2)}) %all-to-all-start) | async-done | bytes 160 | tf_op jit(solution)/shard_map/all_to_all | solution.py:13
  426.8 0.5 reduce_sum.39
  (3 shorter events, 0.0 us)
Async XLA Ops:
  7.2 401.5 %all-reduce.3.cloned.1.call-start = ((), (), s32[]{:S(2)}) async-start(), calls=%async_computation.1 | async-start | bytes 16908288 | tf_op jit(solution)/shard_map/psum | solution.py:62
  412.7 14.1 %all-to-all-start = ((f32[8,1,4]{2,1,0:T(1,128)}), f32[8,1,4]{2,1,0:T(1,128)S(1)}, u32[]{:S(2)}, u32[]{:S(2)}) async-start(f32[8,1,4]{2,1,0:T(1,128)} %broadcast_in_dim.5), calls=%async_computation | async-start | bytes 8192 | tf_op jit(solution)/shard_map/all_to_all | solution.py:13
Sparse Core Ops, SparseCore 0:
  262.8 145.7 all-reduce.2
where the time goes:
time: 437 us; the launch traced here: 434 us
  waiting for transfers between devices  153 us (35%)
  other arithmetic  126 us (29%)
  local copies, waits for them, and re-layouts  112 us (26%)
  matrix products  23.3 us (5%)
  between operations  14.1 us (3%)
  starting transfers between devices  6.45 us (1%)
    psum x1, waiting for transfers between devices, on_device(): summed, counts_all = lax.psum((partial_value, counts), 'stn')  146 us
    convert_element_type x1, other arithmetic, station_beam(): steer_imag = (-amplitude * jnp.sin(phase)).astype(jnp.bfloat16)  63.9 us
    neg x1, other arithmetic, station_beam(): upper = jnp.concatenate((steer_real, -steer_imag), axis=1)  59 us
    unnamed x2, local copies, waits for them, and re-layouts  40.7 us
    reshape x2, local copies, waits for them, and re-layouts, on_device(): partial_value = partial_value.reshape(2, beam_count, -1).transpose(1, 0, 2)  37.3 us
    another operation x1, local copies, waits for them, and re-layouts, station_beam(): signal = volts.reshape(2 * volts.shape[1], chan_local, -1)  26.9 us
    dot_general x1, matrix products, station_beam(): jnp.einsum('pkc,kct->pct', steer_block, signal, preferred_element_type=jn...  23.3 us
  transfers between devices with their start and end apart: 2, of which 2 were waited for; matrix products, arithmetic and copies ran while one was open for 0% of the time, Pallas kernels for 0%

commit v1 on v0

v1 whole, which is shorter than its diff:
```python
import jax
import jax.numpy as jnp
from jax import lax
from jax.experimental import pallas as pl
from jax.experimental.pallas import tpu as pltpu
from jax.sharding import PartitionSpec as P

BLOCK = 128
GROUP = 16
PAD = 128
Y, Z, CORE = 2, 4, 2
PIECES = (1, 1, 1, 1)

def poly(coefs, x):
    total = jnp.full(x.shape, coefs[-1], jnp.float32)
    for c in coefs[-2::-1]:
        total = total * x + c
    return total


def turn(r, terms):
    x = r * r
    return poly(COS7[: terms], x), r * poly(SIN7[: terms], x)


SIN7 = (
    6.283185307136744,
    -41.34170221839102,
    81.60524742222256,
    -76.70580022497265,
    42.057754062457725,
    -15.086565424172946,
    3.781319130391277,
    -0.6207787856421599,
)
COS7 = (
    0.9999999998857545,
    -19.73920874347965,
    64.93938907682282,
    -85.4566583290415,
    60.24213144377024,
    -26.404668561864113,
    7.800131962320425,
    -1.4531123696403512,
)
SINT = (6.283185307179586, -41.34170224039975, 81.60524927607504)
COST = (1.0, -19.739208802178716, 64.93939402266829, -85.45681720669373)


def beam_kernel(
    pos_ref, dir_ref, tap_ref, index_ref, flag_ref, flagv_ref, volt_ref, send_ref, keep_ref,
    buf, sems, t_ref, u_ref, fr_ref, fi_ref, *, start, count, whole,
):
    width = 64 * GROUP
    groups = count // GROUP

    def fetch(g):
        return pltpu.make_async_copy(
            volt_ref.at[0, :, :, pl.ds((start + g * GROUP) * 64, width)],
            buf.at[:, :, pl.ds(g * width, width)],
            sems.at[g],
        )

    for g in range(groups):
        fetch(g).start()

    me = lax.axis_index("stn")
    my_core = me % CORE
    my_z = (me // CORE) % Z
    my_y = me // (CORE * Z)
    rows = lax.broadcasted_iota(jnp.int32, (128, 64), 0)
    tile, sub = rows // 8, rows % 8
    core = jnp.where(tile // 8 == 1, my_core, 1 - my_core)
    y = jnp.where((tile // 4) % 2 == 1, my_y, 1 - my_y)
    order = tile % 4
    shift = jnp.where(order == 0, 2, jnp.where(order == 1, 1, jnp.where(order == 2, 3, 0)))
    z = (my_z + shift) % Z
    beam = y * 32 + z * 8 + core * 4 + sub % 4
    chosen = beam == lax.broadcasted_iota(jnp.int32, (128, 64), 1)

    def column(row):
        return jnp.sum(jnp.where(chosen, row, 0.0), axis=1, keepdims=True)

    weight_row = jnp.zeros((1, 64), jnp.float32)
    for e in range(tap_ref.shape[1]):
        weight_row = weight_row + jnp.where(index_ref[...] == e, tap_ref[0, e], 0.0)
    weight = column(weight_row)
    delay = (
        column(dir_ref[0:1, :]) * pos_ref[0, 0:1, :]
        + column(dir_ref[1:2, :]) * pos_ref[0, 1:2, :]
        + column(dir_ref[2:3, :]) * pos_ref[0, 2:3, :]
    )
    first = lax.axis_index("chan") * (whole // lax.axis_size("chan")) + start
    ratio = 1.0 + 0.5 * (first.astype(jnp.float32) / whole)
    turns = delay * ratio
    cos, sin = turn(turns - jnp.round(turns), 8)
    real = lax.broadcasted_iota(jnp.int32, (128, 256), 0) % 8 < 4
    t_ref[...] = weight * jnp.where(real, cos, -sin)
    u_ref[...] = weight * jnp.where(real, sin, cos)
    step = delay * (0.5 / whole)
    for j in range(GROUP + 1):
        r = step * float(j)
        x = r * r
        fr_ref[j] = poly(COST, x)
        fi_ref[j] = -(r * poly(SINT, x))

    alive = (flagv_ref[0, 0:1, :] + flagv_ref[0, 1:2, :]).astype(jnp.float32) * float(BLOCK)
    lanes = (start // 128) * 128
    share = weight[:, :] * alive[:, lanes : lanes + 128]
    send_ref[:, pl.ds(count * 64, PAD)] = share[:64]
    keep_ref[:, pl.ds(count * 64, PAD)] = share[64:]

    left = lax.broadcasted_iota(jnp.int32, (128, 128), 1) < 64
    sign = jnp.where(lax.broadcasted_iota(jnp.int32, (128, 128), 0) % 8 < 4, -1.0, 1.0)

    def group(g, carry):
        fetch(g).wait()
        t = t_ref[...]
        u = u_ref[...]

        def steer(j):
            value = (t * fr_ref[j] + u * fi_ref[j]).astype(jnp.bfloat16)
            at = start + g * GROUP + j
            halves = []
            for k in range(2):
                keep = flag_ref[0, k, at].astype(jnp.float32)
                keep = jnp.full((128, 128), keep, jnp.float32).astype(jnp.bfloat16)
                halves.append(value[:, 128 * k : 128 * k + 128] * keep)
            return jnp.concatenate(halves, axis=1)

        for p in range(GROUP // 2):
            lhs = jnp.concatenate((steer(2 * p), steer(2 * p + 1)), axis=0)
            at = pl.multiple_of(g * width + p * 128, 128)
            rhs = jnp.concatenate((buf[0, :, pl.ds(at, 128)], buf[1, :, pl.ds(at, 128)]), axis=1)
            both = jnp.dot(lhs, rhs, preferred_element_type=jnp.float32)
            by_real = jnp.where(left, both[:128, :128], both[128:, :128])
            by_imag = jnp.where(left, both[:128, 128:], both[128:, 128:])
            swapped = pltpu.roll(by_imag.reshape(16, 8, 128), 4, 1).reshape(128, 128)
            out = by_real + swapped * sign
            send_ref[:, pl.ds(at, 128)] = out[:64]
            keep_ref[:, pl.ds(at, 128)] = out[64:]
        t_ref[...] = t * fr_ref[GROUP] + u * fi_ref[GROUP]
        u_ref[...] = u * fr_ref[GROUP] - t * fi_ref[GROUP]
        return carry

    lax.fori_loop(0, groups, group, 0)


def core_kernel(keep_ref, got_ref, up_ref, down_ref, rest_ref):
    def block(i):
        return keep_ref[8 * i : 8 * i + 8] + got_ref[8 * i : 8 * i + 8]

    up_ref[0:8] = block(0)
    up_ref[8:16] = block(5)
    down_ref[0:8] = block(4)
    down_ref[8:16] = block(2)
    rest_ref[0:8] = block(1)
    rest_ref[8:16] = block(6)
    rest_ref[16:24] = block(3)
    rest_ref[24:32] = block(7)


def merge_kernel(rest_ref, up_ref, down_ref, up2_ref, down2_ref, own_ref):
    up2_ref[...] = rest_ref[0:8] + up_ref[0:8]
    down2_ref[...] = rest_ref[8:16] + down_ref[0:8]
    own_ref[0:8] = rest_ref[16:24] + down_ref[8:16]
    own_ref[8:16] = rest_ref[24:32] + up_ref[8:16]


def z_kernel(own_ref, up2_ref, down2_ref, send_ref, mine_ref):
    send_ref[...] = own_ref[0:8] + up2_ref[...]
    mine_ref[...] = own_ref[8:16] + down2_ref[...]


def final_kernel(*refs, spans):
    pieces = len(spans)
    mine, got = refs[:pieces], refs[pieces : 2 * pieces]
    power_ref, total_ref = refs[2 * pieces :]
    left = lax.broadcasted_iota(jnp.int32, (8, 128), 1) < 64
    total = jnp.zeros((8, 128), jnp.float32)
    for piece, (start, count) in enumerate(spans):
        counts = mine[piece][:, pl.ds(count * 64, PAD)] + got[piece][:, pl.ds(count * 64, PAD)]
        counts = jnp.where(lax.broadcasted_iota(jnp.int32, (8, 128), 0) < 4, counts, 1.0)
        inside = lax.broadcasted_iota(jnp.int32, (8, 128), 1)
        begin = start % 128
        inside = (inside >= begin) & (inside < begin + count)
        inverse = 1.0 / jnp.where(inside, counts, 1.0)
        for p in range(count // 2):
            value = mine[piece][:, pl.ds(p * 128, 128)] + got[piece][:, pl.ds(p * 128, 128)]
            square = value * value
            square = square + pltpu.roll(square, 4, 0)
            c = begin + 2 * p
            scale = jnp.where(left, inverse[:, c : c + 1], inverse[:, c + 1 : c + 2])
            power = square * (scale * scale)
            power_ref[:, pl.ds(start * 64 + p * 128, 128)] = power[:4]
            total = total + power
    total_ref[...] = jnp.broadcast_to(jnp.sum(total, axis=1, keepdims=True), (8, 128))


def vmem(n):
    return [pl.BlockSpec(memory_space=pltpu.VMEM)] * n


def on_device(voltages, positions, directions, flag_mask, tapers, weight_index):
    chan_local = flag_mask.shape[2]
    whole = chan_local * lax.axis_size("chan")
    unit = chan_local // sum(PIECES)
    spans = []
    for size in PIECES:
        spans.append((sum(s[1] for s in spans), size * unit))

    def number(y, z, core):
        return y * Z * CORE + z % Z * CORE + core

    def pairs(to):
        return [
            (number(y, z, c), number(*to(y, z, c)))
            for y in range(Y) for z in range(Z) for c in range(CORE)
        ]

    to_core = pairs(lambda y, z, c: (y, z, 1 - c))
    to_up = pairs(lambda y, z, c: (y, z + 1, c))
    to_down = pairs(lambda y, z, c: (y, z - 1, c))
    to_y = pairs(lambda y, z, c: (1 - y, z, c))

    def shaped(rows, lanes):
        return jax.ShapeDtypeStruct((rows, lanes), jnp.float32)

    mines, gots = [], []
    for start, count in spans:
        lanes = count * 64 + PAD
        send, keep = pl.pallas_call(
            lambda *refs, start=start, count=count: beam_kernel(
                *refs, start=start, count=count, whole=whole
            ),
            out_shape=(shaped(64, lanes), shaped(64, lanes)),
            in_specs=vmem(2)
            + [pl.BlockSpec(memory_space=pltpu.SMEM)]
            + vmem(1)
            + [pl.BlockSpec(memory_space=pltpu.SMEM)]
            + vmem(1)
            + [pl.BlockSpec(memory_space=pl.ANY)],
            out_specs=tuple(vmem(2)),
            scratch_shapes=[
                pltpu.VMEM((2, 256, count * 64), jnp.bfloat16),
                pltpu.SemaphoreType.DMA((count // GROUP,)),
                pltpu.VMEM((128, 256), jnp.float32),
                pltpu.VMEM((128, 256), jnp.float32),
                pltpu.VMEM((GROUP + 1, 128, 256), jnp.float32),
                pltpu.VMEM((GROUP + 1, 128, 256), jnp.float32),
            ],
            compiler_params=pltpu.CompilerParams(vmem_limit_bytes=24 * 2**20),
            name="beam",
        )(positions, directions, tapers, weight_index, flag_mask, flag_mask, voltages)
        got = lax.ppermute(send, "stn", to_core)
        up, down, rest = pl.pallas_call(
            core_kernel,
            out_shape=(shaped(16, lanes), shaped(16, lanes), shaped(32, lanes)),
            in_specs=vmem(2), out_specs=tuple(vmem(3)), name="core_sum",
        )(keep, got)
        up = lax.ppermute(up, "stn", to_up)
        down = lax.ppermute(down, "stn", to_down)
        up2, down2, own = pl.pallas_call(
            merge_kernel,
            out_shape=(shaped(8, lanes), shaped(8, lanes), shaped(16, lanes)),
            in_specs=vmem(3), out_specs=tuple(vmem(3)), name="merge",
        )(rest, up, down)
        up2 = lax.ppermute(up2, "stn", to_up)
        down2 = lax.ppermute(down2, "stn", to_down)
        over, mine = pl.pallas_call(
            z_kernel,
            out_shape=(shaped(8, lanes), shaped(8, lanes)),
            in_specs=vmem(3), out_specs=tuple(vmem(2)), name="z_sum",
        )(own, up2, down2)
        mines.append(mine)
        gots.append(lax.ppermute(over, "stn", to_y))

    beam_power, total = pl.pallas_call(
        lambda *refs: final_kernel(*refs, spans=spans),
        out_shape=(shaped(4, chan_local * 64), shaped(8, 128)),
        in_specs=vmem(2 * len(spans)), out_specs=tuple(vmem(2)), name="power",
    )(*mines, *gots)
    n = lax.axis_size("chan")
    total = total[:, 0]
    for flip in (1, 3, 4):
        total = total + lax.ppermute(total, "chan", [(i, i ^ flip) for i in range(n)])
    return (beam_power, total[:4])


def solution(mesh):
    in_specs = (
        P("stn", None, None, "chan"),
        P("stn", None, None),
        P(),
        P("stn", None, "chan"),
        P("stn", None),
        P("stn", None),
    )
    out_specs = (P("stn", "chan"), P("stn"))
    return jax.shard_map(
        on_device, mesh=mesh, in_specs=in_specs, out_specs=out_specs, check_vma=False
    )
```

time: 437 us -> 121 us (0.28)
  waiting for transfers between devices: 153 us -> 10.9 us
  other arithmetic: 126 us -> 0.52 us
  local copies, waits for them, and re-layouts: 112 us -> 19.2 us
  Pallas kernels: 0 us -> 51.4 us
  starting transfers between devices: 6.45 us -> 37.5 us
  matrix products: 23.3 us -> 0 us
  between operations: 14.1 us -> 0.89 us
    psum x1 -> x0, waiting for transfers between devices: 146 us -> none  [on_device(): summed, counts_all = lax.psum((partial_value, counts), 'stn')]
    convert_element_type x1 -> x0, other arithmetic: 63.9 us -> none  [station_beam(): steer_imag = (-amplitude * jnp.sin(phase)).astype(jnp.bfloat16)]
    neg x1 -> x0, other arithmetic: 59 us -> none  [station_beam(): upper = jnp.concatenate((steer_real, -steer_imag), axis=1)]
    pallas_call x0 -> x17, Pallas kernels: none -> 51.4 us  [the longest x4 23.2 us: on_device(): pl.pallas_call(lambda *refs, start=start, count=count: beam_kernel(*refs,...]
    reshape x3 -> x0, local copies, waits for them, and re-layouts: 38 us -> none  [the longest x2 37.3 us: on_device(): partial_value = partial_value.reshape(2, beam_count, -1).transpose(1, 0, 2)]
    ppermute x0 -> x27, starting transfers between devices: none -> 37.5 us  [the longest x4 11.8 us: on_device(): down = lax.ppermute(down, 'stn', to_down)]
    another operation x1 -> x0, local copies, waits for them, and re-layouts: 26.9 us -> none  [station_beam(): signal = volts.reshape(2 * volts.shape[1], chan_local, -1)]
    dot_general x1 -> x0, matrix products: 23.3 us -> none  [station_beam(): jnp.einsum('pkc,kct->pct', steer_block, signal, preferred_element_type=jn...]
  transfers between devices with their start and end apart: 2 -> 27, of which waited for: 2 -> 5; matrix products, arithmetic and copies ran while one was open for 0% -> 0% of each run, Pallas kernels for 0% -> 36%
where the time goes in v1:
time: 121 us; the launch traced here: 120 us
  Pallas kernels  51.4 us (42%)
  starting transfers between devices  37.5 us (31%)
  local copies, waits for them, and re-layouts  19.2 us (16%)
  waiting for transfers between devices  10.9 us (9%)
    pallas_call x4, Pallas kernels, on_device(): pl.pallas_call(lambda *refs, start=start, count=count: beam_kernel(*refs,...  23.2 us
    unnamed x65, local copies, waits for them, and re-layouts  18.4 us
    ppermute x4, starting transfers between devices, on_device(): down = lax.ppermute(down, 'stn', to_down)  11.8 us
    ppermute x4, starting transfers between devices, on_device(): down2 = lax.ppermute(down2, 'stn', to_down)  11.1 us
    pallas_call x4, Pallas kernels, on_device(): pl.pallas_call(core_kernel, out_shape=(shaped(16, lanes), shaped(16, lane...  10.4 us
    pallas_call x4, Pallas kernels, on_device(): pl.pallas_call(merge_kernel, out_shape=(shaped(8, lanes), shaped(8, lanes...  8.08 us
    ppermute x3, starting transfers between devices, on_device(): lax.ppermute(total, 'chan', [(i, i ^ flip) for i in range(n)])  7.22 us
    pallas_call x4, Pallas kernels, on_device(): pl.pallas_call(z_kernel, out_shape=(shaped(8, lanes), shaped(8, lanes)),...  7.14 us
  transfers between devices with their start and end apart: 27, of which 5 were waited for; matrix products, arithmetic and copies ran while one was open for 0% of the time, Pallas kernels for 36%

profile of v1, /device:TPU:0, one launch (start us, length us, event | category | flops | bytes accessed | tf_op | source)
XLA Modules:
  0.0 120.5 jit_solution(15719394093105793741)
XLA Ops:
  0.6 0.7 copy.12.refs_0_
  1.3 5.8 %copy-done = bf16[1,2,256,16384]{3,2,1,0:T(8,128)(2,1)S(1)} copy-done((bf16[1,2,256,16384]{3,2,1,0:T(8,128)(2,1)S(1)}, bf16[1,2,256,16384]{3,2,1,0:T(8,128)(2,1)}, u32[]{:S(2)}) %copy-start) | copy-done | bytes 16777240
  7.1 0.7 copy-done.5
  7.8 0.7 copy-done.6
  9.8 5.8 %beam.7 = (f32[64,4224]{1,0:T(8,128)S(1)}, f32[64,4224]{1,0:T(8,128)S(1)}) custom-call(f32[1,3,256]{2,1,0:T(4,128)S(1)} %copy.12.refs_0_, f32[3,64]{1,0:T(4,128)S(1)} %copy-done.6, f32[1,8]{1,0:T(1,128)S(1)} %copy-done.7, s32[1,64]{1,0:T(1,128)S(1)} %copy-done.8, s32[1,2,256]{2,1,0:T(2,128)S(1)} %copy-done.5, s32[1,2,256]{2,1,0:T(2,128)S(1)} %copy-done.5, ...), custom_call_target="tpu_custom_call" | custom-call | tf_op jit(solution)/shard_map/beam/pallas_call | solution.py:232
  15.6 1.1 copy-done.4
  16.6 5.8 %beam.6 = (f32[64,4224]{1,0:T(8,128)S(1)}, f32[64,4224]{1,0:T(8,128)S(1)}) custom-call(f32[1,3,256]{2,1,0:T(4,128)S(1)} %copy.12.refs_0_, f32[3,64]{1,0:T(4,128)S(1)} %copy-done.6, f32[1,8]{1,0:T(1,128)S(1)} %copy-done.7, s32[1,64]{1,0:T(1,128)S(1)} %copy-done.8, s32[1,2,256]{2,1,0:T(2,128)S(1)} %copy-done.5, s32[1,2,256]{2,1,0:T(2,128)S(1)} %copy-done.5, ...), custom_call_target="tpu_custom_call" | custom-call | tf_op jit(solution)/shard_map/beam/pallas_call | solution.py:232
  22.5 1.0 copy-done.3
  24.0 5.8 %beam.5 = (f32[64,4224]{1,0:T(8,128)S(1)}, f32[64,4224]{1,0:T(8,128)S(1)}) custom-call(f32[1,3,256]{2,1,0:T(4,128)S(1)} %copy.12.refs_0_, f32[3,64]{1,0:T(4,128)S(1)} %copy-done.6, f32[1,8]{1,0:T(1,128)S(1)} %copy-done.7, s32[1,64]{1,0:T(1,128)S(1)} %copy-done.8, s32[1,2,256]{2,1,0:T(2,128)S(1)} %copy-done.5, s32[1,2,256]{2,1,0:T(2,128)S(1)} %copy-done.5, ...), custom_call_target="tpu_custom_call" | custom-call | tf_op jit(solution)/shard_map/beam/pallas_call | solution.py:232
  29.8 1.0 copy-done.2
  30.8 5.8 %beam.4 = (f32[64,4224]{1,0:T(8,128)S(1)}, f32[64,4224]{1,0:T(8,128)S(1)}) custom-call(f32[1,3,256]{2,1,0:T(4,128)S(1)} %copy.12.refs_0_, f32[3,64]{1,0:T(4,128)S(1)} %copy-done.6, f32[1,8]{1,0:T(1,128)S(1)} %copy-done.7, s32[1,64]{1,0:T(1,128)S(1)} %copy-done.8, s32[1,2,256]{2,1,0:T(2,128)S(1)} %copy-done.5, s32[1,2,256]{2,1,0:T(2,128)S(1)} %copy-done.5, ...), custom_call_target="tpu_custom_call" | custom-call | tf_op jit(solution)/shard_map/beam/pallas_call | solution.py:232
  36.6 1.0 copy-done.1
  38.2 1.1 copy-done.9
  39.3 2.6 %core_sum.7 = (f32[16,4224]{1,0:T(8,128)}, f32[16,4224]{1,0:T(8,128)}, f32[32,4224]{1,0:T(8,128)}) custom-call(f32[64,4224]{1,0:T(8,128)} %copy-done.4, f32[64,4224]{1,0:T(8,128)} %copy-done.9), custom_call_target="tpu_custom_call" | custom-call | tf_op jit(solution)/shard_map/core_sum/pallas_call | solution.py:256
  41.9 2.0 %collective-permute-start.16 = (f32[16,4224]{1,0:T(8,128)}, f32[16,4224]{1,0:T(8,128)S(1)}, u32[]{:S(2)}, u32[]{:S(2)}) collective-permute-start(f32[16,4224]{1,0:T(8,128)} %get-tuple-element.74), channel_id=1, source_target_pairs={{0,16},{8,24},{16,32},{24,40},{32,48},{40,56},{48,0},{56,8},{64,80... | collective-permute-start | bytes 811016 | tf_op jit(solution)/shard_map/ppermute | solution.py:261
  43.9 2.1 %collective-permute-start.17 = (f32[16,4224]{1,0:T(8,128)}, f32[16,4224]{1,0:T(8,128)}, u32[]{:S(2)}, u32[]{:S(2)}) collective-permute-start(f32[16,4224]{1,0:T(8,128)} %get-tuple-element.75), channel_id=1, source_target_pairs={{0,48},{8,56},{16,0},{24,8},{32,16},{40,24},{48,32},{56,40},{64,11... | collective-permute-start | bytes 811016 | tf_op jit(solution)/shard_map/ppermute | solution.py:262
  46.0 2.6 %core_sum.6 = (f32[16,4224]{1,0:T(8,128)}, f32[16,4224]{1,0:T(8,128)}, f32[32,4224]{1,0:T(8,128)}) custom-call(f32[64,4224]{1,0:T(8,128)} %copy-done.3, f32[64,4224]{1,0:T(8,128)} %collective-permute-done.10.got_ref), custom_call_target="tpu_custom_call" | custom-call | tf_op jit(solution)/shard_map/core_sum/pallas_call | solution.py:256
  48.6 3.2 %collective-permute-start.12 = (f32[16,4224]{1,0:T(8,128)}, f32[16,4224]{1,0:T(8,128)S(1)}, u32[]{:S(2)}, u32[]{:S(2)}) collective-permute-start(f32[16,4224]{1,0:T(8,128)} %get-tuple-element.66), channel_id=1, source_target_pairs={{0,48},{8,56},{16,0},{24,8},{32,16},{40,24},{48,32},{56,40},{64,11... | collective-permute-start | bytes 811016 | tf_op jit(solution)/shard_map/ppermute | solution.py:262
  51.9 2.6 %core_sum.5 = (f32[16,4224]{1,0:T(8,128)}, f32[16,4224]{1,0:T(8,128)}, f32[32,4224]{1,0:T(8,128)}) custom-call(f32[64,4224]{1,0:T(8,128)} %copy-done.2, f32[64,4224]{1,0:T(8,128)} %collective-permute-done.5.got_ref), custom_call_target="tpu_custom_call" | custom-call | tf_op jit(solution)/shard_map/core_sum/pallas_call | solution.py:256
  54.5 3.2 %collective-permute-start.7 = (f32[16,4224]{1,0:T(8,128)}, f32[16,4224]{1,0:T(8,128)S(1)}, u32[]{:S(2)}, u32[]{:S(2)}) collective-permute-start(f32[16,4224]{1,0:T(8,128)} %get-tuple-element.57), channel_id=1, source_target_pairs={{0,48},{8,56},{16,0},{24,8},{32,16},{40,24},{48,32},{56,40},{64,11... | collective-permute-start | bytes 811016 | tf_op jit(solution)/shard_map/ppermute | solution.py:262
  57.8 2.6 %core_sum.4 = (f32[16,4224]{1,0:T(8,128)}, f32[16,4224]{1,0:T(8,128)}, f32[32,4224]{1,0:T(8,128)}) custom-call(f32[64,4224]{1,0:T(8,128)} %copy-done.1, f32[64,4224]{1,0:T(8,128)} %collective-permute-done.got_ref), custom_call_target="tpu_custom_call" | custom-call | tf_op jit(solution)/shard_map/core_sum/pallas_call | solution.py:256
  60.4 3.2 %collective-permute-start.2 = (f32[16,4224]{1,0:T(8,128)}, f32[16,4224]{1,0:T(8,128)S(1)}, u32[]{:S(2)}, u32[]{:S(2)}) collective-permute-start(f32[16,4224]{1,0:T(8,128)} %get-tuple-element.48), channel_id=1, source_target_pairs={{0,48},{8,56},{16,0},{24,8},{32,16},{40,24},{48,32},{56,40},{64,11... | collective-permute-start | bytes 811016 | tf_op jit(solution)/shard_map/ppermute | solution.py:262
  63.6 2.0 %merge.7 = (f32[8,4224]{1,0:T(8,128)}, f32[8,4224]{1,0:T(8,128)}, f32[16,4224]{1,0:T(8,128)}) custom-call(f32[32,4224]{1,0:T(8,128)} %get-tuple-element.73.rest_ref, f32[16,4224]{1,0:T(8,128)} %copy-done.10, f32[16,4224]{1,0:T(8,128)} %collective-permute-done.17.down_ref), custom_call_target="tpu_custom_call" | custom-call | tf_op jit(solution)/shard_map/merge/pallas_call | solution.py:263
  66.4 2.0 %merge.6 = (f32[8,4224]{1,0:T(8,128)}, f32[8,4224]{1,0:T(8,128)}, f32[16,4224]{1,0:T(8,128)}) custom-call(f32[32,4224]{1,0:T(8,128)} %get-tuple-element.64.rest_ref, f32[16,4224]{1,0:T(8,128)} %copy-done.13, f32[16,4224]{1,0:T(8,128)} %copy-done.16), custom_call_target="tpu_custom_call" | custom-call | tf_op jit(solution)/shard_map/merge/pallas_call | solution.py:263
  68.4 2.7 %collective-permute-start.19 = (f32[8,4224]{1,0:T(8,128)S(1)}, f32[8,4224]{1,0:T(8,128)S(1)}, u32[]{:S(2)}, u32[]{:S(2)}) collective-permute-start(f32[8,4224]{1,0:T(8,128)S(1)} %copy-done.31), channel_id=1, source_target_pairs={{0,48},{8,56},{16,0},{24,8},{32,16},{40,24},{48,32},{56,40},{64,11... | collective-permute-start | bytes 405512 | tf_op jit(solution)/shard_map/ppermute | solution.py:269
  71.1 0.7 copy-done.15
  71.8 2.0 %merge.5 = (f32[8,4224]{1,0:T(8,128)}, f32[8,4224]{1,0:T(8,128)}, f32[16,4224]{1,0:T(8,128)}) custom-call(f32[32,4224]{1,0:T(8,128)} %get-tuple-element.55.rest_ref, f32[16,4224]{1,0:T(8,128)} %copy-done.12, f32[16,4224]{1,0:T(8,128)} %copy-done.15), custom_call_target="tpu_custom_call" | custom-call | tf_op jit(solution)/shard_map/merge/pallas_call | solution.py:263
  73.8 2.6 %collective-permute-start.14 = (f32[8,4224]{1,0:T(8,128)S(1)}, f32[8,4224]{1,0:T(8,128)S(1)}, u32[]{:S(2)}, u32[]{:S(2)}) collective-permute-start(f32[8,4224]{1,0:T(8,128)S(1)} %copy-done.29), channel_id=1, source_target_pairs={{0,48},{8,56},{16,0},{24,8},{32,16},{40,24},{48,32},{56,40},{64,11... | collective-permute-start | bytes 405512 | tf_op jit(solution)/shard_map/ppermute | solution.py:269
  76.5 0.7 copy-done.14
  77.2 2.0 %merge.4 = (f32[8,4224]{1,0:T(8,128)}, f32[8,4224]{1,0:T(8,128)}, f32[16,4224]{1,0:T(8,128)}) custom-call(f32[32,4224]{1,0:T(8,128)} %get-tuple-element.46.rest_ref, f32[16,4224]{1,0:T(8,128)} %copy-done.11, f32[16,4224]{1,0:T(8,128)} %copy-done.14), custom_call_target="tpu_custom_call" | custom-call | tf_op jit(solution)/shard_map/merge/pallas_call | solution.py:263
  79.2 2.6 %collective-permute-start.9 = (f32[8,4224]{1,0:T(8,128)S(1)}, f32[8,4224]{1,0:T(8,128)S(1)}, u32[]{:S(2)}, u32[]{:S(2)}) collective-permute-start(f32[8,4224]{1,0:T(8,128)S(1)} %copy-done.30), channel_id=1, source_target_pairs={{0,48},{8,56},{16,0},{24,8},{32,16},{40,24},{48,32},{56,40},{64,11... | collective-permute-start | bytes 405512 | tf_op jit(solution)/shard_map/ppermute | solution.py:269
  81.8 3.2 %collective-permute-start.4 = (f32[8,4224]{1,0:T(8,128)}, f32[8,4224]{1,0:T(8,128)S(1)}, u32[]{:S(2)}, u32[]{:S(2)}) collective-permute-start(f32[8,4224]{1,0:T(8,128)} %get-tuple-element.51), channel_id=1, source_target_pairs={{0,48},{8,56},{16,0},{24,8},{32,16},{40,24},{48,32},{56,40},{64,11... | collective-permute-start | bytes 405512 | tf_op jit(solution)/shard_map/ppermute | solution.py:269
  85.0 1.8 %z_sum.7 = (f32[8,4224]{1,0:T(8,128)}, f32[8,4224]{1,0:T(8,128)}) custom-call(f32[16,4224]{1,0:T(8,128)} %get-tuple-element.76.own_ref, f32[8,4224]{1,0:T(8,128)} %copy-done.21, f32[8,4224]{1,0:T(8,128)} %copy-done.24), custom_call_target="tpu_custom_call" | custom-call | tf_op jit(solution)/shard_map/z_sum/pallas_call | solution.py:270
  86.8 1.6 %collective-permute-start.23 = (f32[8,4224]{1,0:T(8,128)}, f32[8,4224]{1,0:T(8,128)S(1)}, u32[]{:S(2)}, u32[]{:S(2)}) collective-permute-start(f32[8,4224]{1,0:T(8,128)} %get-tuple-element.83), channel_id=1, source_target_pairs={{0,64},{8,72},{16,80},{24,88},{32,96},{40,104},{48,112},{56,120},{... | collective-permute-start | bytes 405512 | tf_op jit(solution)/shard_map/ppermute | solution.py:276
  88.4 1.8 %z_sum.6 = (f32[8,4224]{1,0:T(8,128)}, f32[8,4224]{1,0:T(8,128)}) custom-call(f32[16,4224]{1,0:T(8,128)} %get-tuple-element.67.own_ref, f32[8,4224]{1,0:T(8,128)} %copy-done.22, f32[8,4224]{1,0:T(8,128)} %copy-done.26), custom_call_target="tpu_custom_call" | custom-call | tf_op jit(solution)/shard_map/z_sum/pallas_call | solution.py:270
  91.5 1.8 %z_sum.5 = (f32[8,4224]{1,0:T(8,128)}, f32[8,4224]{1,0:T(8,128)}) custom-call(f32[16,4224]{1,0:T(8,128)} %get-tuple-element.58.own_ref, f32[8,4224]{1,0:T(8,128)} %copy-done.23, f32[8,4224]{1,0:T(8,128)} %copy-done.28), custom_call_target="tpu_custom_call" | custom-call | tf_op jit(solution)/shard_map/z_sum/pallas_call | solution.py:270
  93.3 1.4 %collective-permute-start.21 = (f32[8,4224]{1,0:T(8,128)}, f32[8,4224]{1,0:T(8,128)S(1)}, u32[]{:S(2)}, u32[]{:S(2)}) collective-permute-start(f32[8,4224]{1,0:T(8,128)} %get-tuple-element.81), channel_id=1, source_target_pairs={{0,64},{8,72},{16,80},{24,88},{32,96},{40,104},{48,112},{56,120},{... | collective-permute-start | bytes 405512 | tf_op jit(solution)/shard_map/ppermute | solution.py:276
  95.5 1.8 %z_sum.4 = (f32[8,4224]{1,0:T(8,128)}, f32[8,4224]{1,0:T(8,128)}) custom-call(f32[16,4224]{1,0:T(8,128)} %get-tuple-element.49.own_ref, f32[8,4224]{1,0:T(8,128)} %copy-done.25, f32[8,4224]{1,0:T(8,128)} %copy-done.27), custom_call_target="tpu_custom_call" | custom-call | tf_op jit(solution)/shard_map/z_sum/pallas_call | solution.py:270
  97.9 0.7 collective-permute-done.21.refs_5_
  98.6 3.9 %collective-permute-done.20.refs_4_ = f32[8,4224]{1,0:T(8,128)S(1)} collective-permute-done((f32[8,4224]{1,0:T(8,128)}, f32[8,4224]{1,0:T(8,128)S(1)}, u32[]{:S(2)}, u32[]{:S(2)}) %collective-permute-start.20) | collective-permute-done | bytes 135200 | tf_op jit(solution)/shard_map/ppermute | solution.py:276
  103.1 2.5 %power.1 = (f32[4,16384]{1,0:T(4,128)}, f32[8,128]{1,0:T(8,128)}) custom-call(f32[8,4224]{1,0:T(8,128)} %get-tuple-element.52.refs_0_, f32[8,4224]{1,0:T(8,128)} %get-tuple-element.61.refs_1_, f32[8,4224]{1,0:T(8,128)} %get-tuple-element.70.refs_2_, f32[8,4224]{1,0:T(8,128)} %get-tuple-element.79.refs_3_, f32[8,4224]{1,0:T(8,128)} %copy-done.20, ...), custom_call_target="tpu_custom_call" | custom-call | tf_op jit(solution)/shard_map/power/pallas_call | solution.py:278
  105.6 0.8 slice_reduce_fusion
  106.4 1.6 %collective-permute-start.24 = (f32[8]{0:T(128)S(1)}, f32[8]{0:T(128)S(1)}, u32[]{:S(2)}, u32[]{:S(2)}) collective-permute-start(f32[8]{0:T(128)S(1)} %slice_reduce_fusion), channel_id=1, source_target_pairs={{0,1},{1,0},{2,3},{3,2},{4,5},{5,4},{6,7},{7,6},{8,9},{9,8},{10,11... | collective-permute-start | bytes 104 | tf_op jit(solution)/shard_map/ppermute | solution.py:286
  108.0 2.1 %collective-permute-done.24 = f32[8]{0:T(128)S(1)} collective-permute-done((f32[8]{0:T(128)S(1)}, f32[8]{0:T(128)S(1)}, u32[]{:S(2)}, u32[]{:S(2)}) %collective-permute-start.24) | collective-permute-done | bytes 64 | tf_op jit(solution)/shard_map/ppermute | solution.py:286
  110.1 2.8 %collective-permute-start.25 = (f32[8]{0:T(128)S(1)}, f32[8]{0:T(128)S(1)}, u32[]{:S(2)}, u32[]{:S(2)}) collective-permute-start(f32[8]{0:T(128)S(1)} %add.9), channel_id=1, source_target_pairs={{0,3},{1,2},{2,1},{3,0},{4,7},{5,6},{6,5},{7,4},{8,11},{9,10},{10,... | collective-permute-start | bytes 104 | tf_op jit(solution)/shard_map/ppermute | solution.py:286
  112.8 2.0 %collective-permute-done.25 = f32[8]{0:T(128)S(1)} collective-permute-done((f32[8]{0:T(128)S(1)}, f32[8]{0:T(128)S(1)}, u32[]{:S(2)}, u32[]{:S(2)}) %collective-permute-start.25) | collective-permute-done | bytes 64 | tf_op jit(solution)/shard_map/ppermute | solution.py:286
  114.9 2.9 %collective-permute-start.26 = (f32[8]{0:T(128)S(1)}, f32[8]{0:T(128)S(1)}, u32[]{:S(2)}, u32[]{:S(2)}) collective-permute-start(f32[8]{0:T(128)S(1)} %add.10), channel_id=1, source_target_pairs={{0,4},{1,5},{2,6},{3,7},{4,0},{5,1},{6,2},{7,3},{8,12},{9,13},{10,... | collective-permute-start | bytes 104 | tf_op jit(solution)/shard_map/ppermute | solution.py:286
  117.8 2.2 %collective-permute-done.26 = f32[8]{0:T(128)S(1)} collective-permute-done((f32[8]{0:T(128)S(1)}, f32[8]{0:T(128)S(1)}, u32[]{:S(2)}, u32[]{:S(2)}) %collective-permute-start.26) | collective-permute-done | bytes 64 | tf_op jit(solution)/shard_map/ppermute | solution.py:286
  (92 shorter events, 6.9 us)
Async XLA Ops:
  1.3 5.8 %copy-start = (bf16[1,2,256,16384]{3,2,1,0:T(8,128)(2,1)S(1)}, bf16[1,2,256,16384]{3,2,1,0:T(8,128)(2,1)}, u32[]{:S(2)}) copy-start(bf16[1,2,256,16384]{3,2,1,0:T(8,128)(2,1)} %refs_6_.7) | copy-start | bytes 50331652
  15.6 1.1 copy-start.4
  16.6 21.5 %collective-permute-start.15 = (f32[64,4224]{1,0:T(8,128)S(1)}, f32[64,4224]{1,0:T(8,128)S(1)}, u32[]{:S(2)}, u32[]{:S(2)}) collective-permute-start(f32[64,4224]{1,0:T(8,128)S(1)} %get-tuple-element.72), channel_id=1, source_target_pairs={{0,8},{8,0},{16,24},{24,16},{32,40},{40,32},{48,56},{56,48},{64,72... | collective-permute-start | bytes 3244040 | tf_op jit(solution)/shard_map/ppermute | solution.py:255
  22.5 1.0 copy-start.3
  23.5 22.6 %collective-permute-start.10 = (f32[64,4224]{1,0:T(8,128)S(1)}, f32[64,4224]{1,0:T(8,128)}, u32[]{:S(2)}, u32[]{:S(2)}) collective-permute-start(f32[64,4224]{1,0:T(8,128)S(1)} %get-tuple-element.63), channel_id=1, source_target_pairs={{0,8},{8,0},{16,24},{24,16},{32,40},{40,32},{48,56},{56,48},{64,72... | collective-permute-start | bytes 3244040 | tf_op jit(solution)/shard_map/ppermute | solution.py:255
  29.8 1.0 copy-start.2
  30.8 17.8 %collective-permute-start.5 = (f32[64,4224]{1,0:T(8,128)S(1)}, f32[64,4224]{1,0:T(8,128)}, u32[]{:S(2)}, u32[]{:S(2)}) collective-permute-start(f32[64,4224]{1,0:T(8,128)S(1)} %get-tuple-element.54), channel_id=1, source_target_pairs={{0,8},{8,0},{16,24},{24,16},{32,40},{40,32},{48,56},{56,48},{64,72... | collective-permute-start | bytes 3244040 | tf_op jit(solution)/shard_map/ppermute | solution.py:255
  36.6 1.0 copy-start.1
  37.7 16.9 %collective-permute-start = (f32[64,4224]{1,0:T(8,128)S(1)}, f32[64,4224]{1,0:T(8,128)}, u32[]{:S(2)}, u32[]{:S(2)}) collective-permute-start(f32[64,4224]{1,0:T(8,128)S(1)} %get-tuple-element.45), channel_id=1, source_target_pairs={{0,8},{8,0},{16,24},{24,16},{32,40},{40,32},{48,56},{56,48},{64,72... | collective-permute-start | bytes 3244040 | tf_op jit(solution)/shard_map/ppermute | solution.py:255
  38.2 1.1 copy-start.9
  41.9 12.6 %collective-permute-start.16 = (f32[16,4224]{1,0:T(8,128)}, f32[16,4224]{1,0:T(8,128)S(1)}, u32[]{:S(2)}, u32[]{:S(2)}) collective-permute-start(f32[16,4224]{1,0:T(8,128)} %get-tuple-element.74), channel_id=1, source_target_pairs={{0,16},{8,24},{16,32},{24,40},{32,48},{40,56},{48,0},{56,8},{64,80... | collective-permute-start | bytes 811016 | tf_op jit(solution)/shard_map/ppermute | solution.py:261
  43.9 16.4 %collective-permute-start.17 = (f32[16,4224]{1,0:T(8,128)}, f32[16,4224]{1,0:T(8,128)}, u32[]{:S(2)}, u32[]{:S(2)}) collective-permute-start(f32[16,4224]{1,0:T(8,128)} %get-tuple-element.75), channel_id=1, source_target_pairs={{0,48},{8,56},{16,0},{24,8},{32,16},{40,24},{48,32},{56,40},{64,11... | collective-permute-start | bytes 811016 | tf_op jit(solution)/shard_map/ppermute | solution.py:262
  48.6 11.8 %collective-permute-start.11 = (f32[16,4224]{1,0:T(8,128)}, f32[16,4224]{1,0:T(8,128)S(1)}, u32[]{:S(2)}, u32[]{:S(2)}) collective-permute-start(f32[16,4224]{1,0:T(8,128)} %get-tuple-element.65), channel_id=1, source_target_pairs={{0,16},{8,24},{16,32},{24,40},{32,48},{40,56},{48,0},{56,8},{64,80... | collective-permute-start | bytes 811016 | tf_op jit(solution)/shard_map/ppermute | solution.py:261
  48.6 17.0 %collective-permute-start.12 = (f32[16,4224]{1,0:T(8,128)}, f32[16,4224]{1,0:T(8,128)S(1)}, u32[]{:S(2)}, u32[]{:S(2)}) collective-permute-start(f32[16,4224]{1,0:T(8,128)} %get-tuple-element.66), channel_id=1, source_target_pairs={{0,48},{8,56},{16,0},{24,8},{32,16},{40,24},{48,32},{56,40},{64,11... | collective-permute-start | bytes 811016 | tf_op jit(solution)/shard_map/ppermute | solution.py:262
  54.5 13.9 %collective-permute-start.6 = (f32[16,4224]{1,0:T(8,128)}, f32[16,4224]{1,0:T(8,128)S(1)}, u32[]{:S(2)}, u32[]{:S(2)}) collective-permute-start(f32[16,4224]{1,0:T(8,128)} %get-tuple-element.56), channel_id=1, source_target_pairs={{0,16},{8,24},{16,32},{24,40},{32,48},{40,56},{48,0},{56,8},{64,80... | collective-permute-start | bytes 811016 | tf_op jit(solution)/shard_map/ppermute | solution.py:261
  54.5 5.8 %copy-start.10 = (f32[16,4224]{1,0:T(8,128)}, f32[16,4224]{1,0:T(8,128)S(1)}, u32[]{:S(2)}) copy-start(f32[16,4224]{1,0:T(8,128)S(1)} %collective-permute-done.16.up_ref) | copy-start | bytes 811012
  54.5 16.5 %collective-permute-start.7 = (f32[16,4224]{1,0:T(8,128)}, f32[16,4224]{1,0:T(8,128)S(1)}, u32[]{:S(2)}, u32[]{:S(2)}) collective-permute-start(f32[16,4224]{1,0:T(8,128)} %get-tuple-element.57), channel_id=1, source_target_pairs={{0,48},{8,56},{16,0},{24,8},{32,16},{40,24},{48,32},{56,40},{64,11... | collective-permute-start | bytes 811016 | tf_op jit(solution)/shard_map/ppermute | solution.py:262
  60.4 13.5 %collective-permute-start.1 = (f32[16,4224]{1,0:T(8,128)}, f32[16,4224]{1,0:T(8,128)S(1)}, u32[]{:S(2)}, u32[]{:S(2)}) collective-permute-start(f32[16,4224]{1,0:T(8,128)} %get-tuple-element.47), channel_id=1, source_target_pairs={{0,16},{8,24},{16,32},{24,40},{32,48},{40,56},{48,0},{56,8},{64,80... | collective-permute-start | bytes 811016 | tf_op jit(solution)/shard_map/ppermute | solution.py:261
  60.4 5.4 %copy-start.13 = (f32[16,4224]{1,0:T(8,128)}, f32[16,4224]{1,0:T(8,128)S(1)}, u32[]{:S(2)}) copy-start(f32[16,4224]{1,0:T(8,128)S(1)} %collective-permute-done.11.up_ref) | copy-start | bytes 811012
  60.4 16.0 %collective-permute-start.2 = (f32[16,4224]{1,0:T(8,128)}, f32[16,4224]{1,0:T(8,128)S(1)}, u32[]{:S(2)}, u32[]{:S(2)}) collective-permute-start(f32[16,4224]{1,0:T(8,128)} %get-tuple-element.48), channel_id=1, source_target_pairs={{0,48},{8,56},{16,0},{24,8},{32,16},{40,24},{48,32},{56,40},{64,11... | collective-permute-start | bytes 811016 | tf_op jit(solution)/shard_map/ppermute | solution.py:262
  65.7 2.7 %copy-start.31 = (f32[8,4224]{1,0:T(8,128)S(1)}, f32[8,4224]{1,0:T(8,128)}, u32[]{:S(2)}) copy-start(f32[8,4224]{1,0:T(8,128)} %get-tuple-element.78) | copy-start | bytes 405508
  65.7 0.7 copy-start.16
  65.7 13.5 %collective-permute-start.18 = (f32[8,4224]{1,0:T(8,128)}, f32[8,4224]{1,0:T(8,128)S(1)}, u32[]{:S(2)}, u32[]{:S(2)}) collective-permute-start(f32[8,4224]{1,0:T(8,128)} %get-tuple-element.77), channel_id=1, source_target_pairs={{0,16},{8,24},{16,32},{24,40},{32,48},{40,56},{48,0},{56,8},{64,80... | collective-permute-start | bytes 405512 | tf_op jit(solution)/shard_map/ppermute | solution.py:268
  68.4 5.4 %copy-start.29 = (f32[8,4224]{1,0:T(8,128)S(1)}, f32[8,4224]{1,0:T(8,128)}, u32[]{:S(2)}) copy-start(f32[8,4224]{1,0:T(8,128)} %get-tuple-element.69) | copy-start | bytes 405508
  68.4 2.7 %copy-start.12 = (f32[16,4224]{1,0:T(8,128)}, f32[16,4224]{1,0:T(8,128)S(1)}, u32[]{:S(2)}) copy-start(f32[16,4224]{1,0:T(8,128)S(1)} %collective-permute-done.6.up_ref) | copy-start | bytes 811012
  68.4 13.4 %collective-permute-start.19 = (f32[8,4224]{1,0:T(8,128)S(1)}, f32[8,4224]{1,0:T(8,128)S(1)}, u32[]{:S(2)}, u32[]{:S(2)}) collective-permute-start(f32[8,4224]{1,0:T(8,128)S(1)} %copy-done.31), channel_id=1, source_target_pairs={{0,48},{8,56},{16,0},{24,8},{32,16},{40,24},{48,32},{56,40},{64,11... | collective-permute-start | bytes 405512 | tf_op jit(solution)/shard_map/ppermute | solution.py:269
  71.1 10.7 %collective-permute-start.13 = (f32[8,4224]{1,0:T(8,128)}, f32[8,4224]{1,0:T(8,128)S(1)}, u32[]{:S(2)}, u32[]{:S(2)}) collective-permute-start(f32[8,4224]{1,0:T(8,128)} %get-tuple-element.68), channel_id=1, source_target_pairs={{0,16},{8,24},{16,32},{24,40},{32,48},{40,56},{48,0},{56,8},{64,80... | collective-permute-start | bytes 405512 | tf_op jit(solution)/shard_map/ppermute | solution.py:268
  73.8 5.4 %copy-start.30 = (f32[8,4224]{1,0:T(8,128)S(1)}, f32[8,4224]{1,0:T(8,128)}, u32[]{:S(2)}) copy-start(f32[8,4224]{1,0:T(8,128)} %get-tuple-element.60) | copy-start | bytes 405508
  73.8 2.6 %copy-start.11 = (f32[16,4224]{1,0:T(8,128)}, f32[16,4224]{1,0:T(8,128)S(1)}, u32[]{:S(2)}) copy-start(f32[16,4224]{1,0:T(8,128)S(1)} %collective-permute-done.1.up_ref) | copy-start | bytes 811012
  73.8 13.0 %collective-permute-start.14 = (f32[8,4224]{1,0:T(8,128)S(1)}, f32[8,4224]{1,0:T(8,128)S(1)}, u32[]{:S(2)}, u32[]{:S(2)}) collective-permute-start(f32[8,4224]{1,0:T(8,128)S(1)} %copy-done.29), channel_id=1, source_target_pairs={{0,48},{8,56},{16,0},{24,8},{32,16},{40,24},{48,32},{56,40},{64,11... | collective-permute-start | bytes 405512 | tf_op jit(solution)/shard_map/ppermute | solution.py:269
  76.4 13.8 %collective-permute-start.8 = (f32[8,4224]{1,0:T(8,128)}, f32[8,4224]{1,0:T(8,128)S(1)}, u32[]{:S(2)}, u32[]{:S(2)}) collective-permute-start(f32[8,4224]{1,0:T(8,128)} %get-tuple-element.59), channel_id=1, source_target_pairs={{0,16},{8,24},{16,32},{24,40},{32,48},{40,56},{48,0},{56,8},{64,80... | collective-permute-start | bytes 405512 | tf_op jit(solution)/shard_map/ppermute | solution.py:268
  79.2 5.9 %copy-start.21 = (f32[8,4224]{1,0:T(8,128)}, f32[8,4224]{1,0:T(8,128)S(1)}, u32[]{:S(2)}) copy-start(f32[8,4224]{1,0:T(8,128)S(1)} %collective-permute-done.18.up2_ref) | copy-start | bytes 405508
  79.2 11.7 %collective-permute-start.9 = (f32[8,4224]{1,0:T(8,128)S(1)}, f32[8,4224]{1,0:T(8,128)S(1)}, u32[]{:S(2)}, u32[]{:S(2)}) collective-permute-start(f32[8,4224]{1,0:T(8,128)S(1)} %copy-done.30), channel_id=1, source_target_pairs={{0,48},{8,56},{16,0},{24,8},{32,16},{40,24},{48,32},{56,40},{64,11... | collective-permute-start | bytes 405512 | tf_op jit(solution)/shard_map/ppermute | solution.py:269
  81.8 3.3 %copy-start.24 = (f32[8,4224]{1,0:T(8,128)}, f32[8,4224]{1,0:T(8,128)S(1)}, u32[]{:S(2)}) copy-start(f32[8,4224]{1,0:T(8,128)S(1)} %collective-permute-done.19.down2_ref) | copy-start | bytes 405508
  81.8 13.0 %collective-permute-start.3 = (f32[8,4224]{1,0:T(8,128)}, f32[8,4224]{1,0:T(8,128)S(1)}, u32[]{:S(2)}, u32[]{:S(2)}) collective-permute-start(f32[8,4224]{1,0:T(8,128)} %get-tuple-element.50), channel_id=1, source_target_pairs={{0,16},{8,24},{16,32},{24,40},{32,48},{40,56},{48,0},{56,8},{64,80... | collective-permute-start | bytes 405512 | tf_op jit(solution)/shard_map/ppermute | solution.py:268
  81.8 6.6 %copy-start.22 = (f32[8,4224]{1,0:T(8,128)}, f32[8,4224]{1,0:T(8,128)S(1)}, u32[]{:S(2)}) copy-start(f32[8,4224]{1,0:T(8,128)S(1)} %collective-permute-done.13.up2_ref) | copy-start | bytes 405508
  81.8 13.0 %collective-permute-start.4 = (f32[8,4224]{1,0:T(8,128)}, f32[8,4224]{1,0:T(8,128)S(1)}, u32[]{:S(2)}, u32[]{:S(2)}) collective-permute-start(f32[8,4224]{1,0:T(8,128)} %get-tuple-element.51), channel_id=1, source_target_pairs={{0,48},{8,56},{16,0},{24,8},{32,16},{40,24},{48,32},{56,40},{64,11... | collective-permute-start | bytes 405512 | tf_op jit(solution)/shard_map/ppermute | solution.py:269
  86.8 1.6 %copy-start.26 = (f32[8,4224]{1,0:T(8,128)}, f32[8,4224]{1,0:T(8,128)S(1)}, u32[]{:S(2)}) copy-start(f32[8,4224]{1,0:T(8,128)S(1)} %collective-permute-done.14.down2_ref) | copy-start | bytes 405508
  86.8 11.0 %collective-permute-start.23 = (f32[8,4224]{1,0:T(8,128)}, f32[8,4224]{1,0:T(8,128)S(1)}, u32[]{:S(2)}, u32[]{:S(2)}) collective-permute-start(f32[8,4224]{1,0:T(8,128)} %get-tuple-element.83), channel_id=1, source_target_pairs={{0,64},{8,72},{16,80},{24,88},{32,96},{40,104},{48,112},{56,120},{... | collective-permute-start | bytes 405512 | tf_op jit(solution)/shard_map/ppermute | solution.py:276
  90.2 7.6 %collective-permute-start.22 = (f32[8,4224]{1,0:T(8,128)}, f32[8,4224]{1,0:T(8,128)S(1)}, u32[]{:S(2)}, u32[]{:S(2)}) collective-permute-start(f32[8,4224]{1,0:T(8,128)} %get-tuple-element.82), channel_id=1, source_target_pairs={{0,64},{8,72},{16,80},{24,88},{32,96},{40,104},{48,112},{56,120},{... | collective-permute-start | bytes 405512 | tf_op jit(solution)/shard_map/ppermute | solution.py:276
  93.3 5.2 %collective-permute-start.21 = (f32[8,4224]{1,0:T(8,128)}, f32[8,4224]{1,0:T(8,128)S(1)}, u32[]{:S(2)}, u32[]{:S(2)}) collective-permute-start(f32[8,4224]{1,0:T(8,128)} %get-tuple-element.81), channel_id=1, source_target_pairs={{0,64},{8,72},{16,80},{24,88},{32,96},{40,104},{48,112},{56,120},{... | collective-permute-start | bytes 405512 | tf_op jit(solution)/shard_map/ppermute | solution.py:276
  97.2 5.2 %collective-permute-start.20 = (f32[8,4224]{1,0:T(8,128)}, f32[8,4224]{1,0:T(8,128)S(1)}, u32[]{:S(2)}, u32[]{:S(2)}) collective-permute-start(f32[8,4224]{1,0:T(8,128)} %get-tuple-element.80), channel_id=1, source_target_pairs={{0,64},{8,72},{16,80},{24,88},{32,96},{40,104},{48,112},{56,120},{... | collective-permute-start | bytes 405512 | tf_op jit(solution)/shard_map/ppermute | solution.py:276
  97.8 4.6 %copy-start.17 = (f32[8,4224]{1,0:T(8,128)}, f32[8,4224]{1,0:T(8,128)S(1)}, u32[]{:S(2)}) copy-start(f32[8,4224]{1,0:T(8,128)S(1)} %collective-permute-done.23.refs_7_) | copy-start | bytes 405508
  97.9 4.6 %copy-start.18 = (f32[8,4224]{1,0:T(8,128)}, f32[8,4224]{1,0:T(8,128)S(1)}, u32[]{:S(2)}) copy-start(f32[8,4224]{1,0:T(8,128)S(1)} %collective-permute-done.22.refs_6_) | copy-start | bytes 405508
  98.6 3.9 %copy-start.19 = (f32[8,4224]{1,0:T(8,128)}, f32[8,4224]{1,0:T(8,128)S(1)}, u32[]{:S(2)}) copy-start(f32[8,4224]{1,0:T(8,128)S(1)} %collective-permute-done.21.refs_5_) | copy-start | bytes 405508
  106.4 3.6 %collective-permute-start.24 = (f32[8]{0:T(128)S(1)}, f32[8]{0:T(128)S(1)}, u32[]{:S(2)}, u32[]{:S(2)}) collective-permute-start(f32[8]{0:T(128)S(1)} %slice_reduce_fusion), channel_id=1, source_target_pairs={{0,1},{1,0},{2,3},{3,2},{4,5},{5,4},{6,7},{7,6},{8,9},{9,8},{10,11... | collective-permute-start | bytes 104 | tf_op jit(solution)/shard_map/ppermute | solution.py:286
  110.1 4.8 %collective-permute-start.25 = (f32[8]{0:T(128)S(1)}, f32[8]{0:T(128)S(1)}, u32[]{:S(2)}, u32[]{:S(2)}) collective-permute-start(f32[8]{0:T(128)S(1)} %add.9), channel_id=1, source_target_pairs={{0,3},{1,2},{2,1},{3,0},{4,7},{5,6},{6,5},{7,4},{8,11},{9,10},{10,... | collective-permute-start | bytes 104 | tf_op jit(solution)/shard_map/ppermute | solution.py:286
  114.9 5.1 %collective-permute-start.26 = (f32[8]{0:T(128)S(1)}, f32[8]{0:T(128)S(1)}, u32[]{:S(2)}, u32[]{:S(2)}) collective-permute-start(f32[8]{0:T(128)S(1)} %add.10), channel_id=1, source_target_pairs={{0,4},{1,5},{2,6},{3,7},{4,0},{5,1},{6,2},{7,3},{8,12},{9,13},{10,... | collective-permute-start | bytes 104 | tf_op jit(solution)/shard_map/ppermute | solution.py:286
  (11 other events, 7.4 us)
